TPU v7x, 128 devices: a 2x2x16 block of a 8x8x16 slice. The times are simulated.
128 devices in a mesh: grp: 4 (over x, y), seq: 32 (over z, core).
Axes of the slice: x: 2, y: 2, z: 16, core: 2. Of those that a mesh axis runs over, the one named last changes fastest.
The devices are a block of a 8x8x16 slice.
Arguments:
- cont_query: bfloat16 [256, 32, 2560], P(('grp', 'seq')), parts along dimension 0, may hold values from -180 to 180
- cont_key: bfloat16 [256, 32, 512], P(('grp', 'seq')), parts along dimension 0, may hold values from -6 to 6
- cont_value: bfloat16 [256, 32, 512], P(('grp', 'seq')), parts along dimension 0, may hold values from -6 to 6
- prefix_key: bfloat16 [16, 2048, 512], P('grp', 'seq'), parts along dimension 0, may hold values from -7 to 7
- prefix_value: bfloat16 [16, 2048, 512], P('grp', 'seq'), parts along dimension 0, may hold values from -6 to 6
- out_weight: bfloat16 [2560, 2560], P(None, 'seq'), may hold values from -0.125 to 0.125
- norm_gain: float32 [2560], replicated, may hold values from 0.5 to 1.5
- lm_head: bfloat16 [2560, 76032], P(None, 'seq'), may hold values from -18 to 18
- target_ids: int32 [256, 32], P(('grp', 'seq')), parts along dimension 0, may hold values from 0 to 76031
- cont_len: int32 [256], P(('grp', 'seq')), parts along dimension 0, may hold values from 8 to 32
- prompt_len: int32 [16], P('grp'), parts along dimension 0, may hold values from 1024 to 2048
- group_of: int32 [256], P('grp'), parts along dimension 0, may hold values from 0 to 3, as said below
- rewards: float32 [256], P(('grp', 'seq')), parts along dimension 0, may hold values from -13 to 13
Outputs:
- token_logprob: float32 [256, 32], P(('grp', 'seq')), parts along dimension 0
- advantage: float32 [256], P(('grp', 'seq')), parts along dimension 0
- objective: float32 [256], P(('grp', 'seq')), parts along dimension 0
There are 4 independent parts, one for each index of `grp`. A program takes and returns all parts, laid end to end along the dimension named above; an argument that names none is the same for every part. Nothing has to cross between parts.
Inputs may be any that keep to these rules, and one draw needn't show every extreme that they name: `group_of`: each of the 4 prompts is named by exactly 16 continuations.
All inputs are finite; a program needn't handle non-finite values.
Results may differ from a plain program's by a relative error of at most 0.0026.
Values may be sent and summed in bfloat16 or wider, within the bound.
A program may use at most 128 MiB of HBM per device.

v0:
```python
import jax
import jax.numpy as jnp
from jax import lax
from jax.sharding import Mesh
from jax.sharding import PartitionSpec as P

HD = 128
GROUP = 16
SEQ = ("seq_0", "seq_1")
GRP_SEQ = ("grp", "seq_0", "seq_1")


NEGATIVE = -1e30
EPSILON = 1e-06
REWARD_FLOOR = 0.25


def sent_together(arrays, axis, dim, along):
    widths = [a.shape[along] for a in arrays]
    both = jnp.concatenate(arrays, axis=along)
    whole = lax.all_gather(both, axis, axis=dim, tiled=True)
    return tuple(jnp.split(whole, [sum(widths[:k]) for k in range(1, len(widths))], axis=along))


def gathered_once(shard, axis):
    leaves = jax.tree.leaves(shard)
    order = sorted(range(len(leaves)), key=lambda k: -leaves[k].size)
    width = (1, *leaves[order[0]].shape)[-1]
    lines = [
        jnp.pad(leaves[k].reshape(-1), (0, -leaves[k].size % width)).reshape(-1, width)
        for k in order
    ]
    both, at, found = (lax.all_gather(jnp.concatenate(lines), axis), 0, {})
    for k, line in zip(order, lines):
        piece = both[:, at : at + len(line)].reshape(len(both), -1)
        found[k] = piece[:, : leaves[k].size].reshape(-1, *leaves[k].shape)
        at += len(line)
    numbers = iter(range(len(leaves)))
    return jax.tree.map(lambda _: found[next(numbers)], shard)


def joined_all(shard, axes, combine):
    for axis in axes:
        pieces = gathered_once(shard, axis)
        shard = jax.tree.map(lambda part: part[0], pieces)
        for k in range(1, lax.axis_size(axis)):
            shard = combine(shard, jax.tree.map(lambda part: part[k], pieces))
    return shard


def absorb(running, queries, key_rows, value_rows, visible):
    peak_old, sum_old, acc_old = running
    cont_count, length, kv_width = key_rows.shape
    head_count = kv_width // HD
    key_heads = key_rows.reshape(cont_count, length, head_count, HD)
    value_heads = value_rows.reshape(cont_count, length, head_count, HD).astype(jnp.float32)
    scores = jnp.einsum(
        "ctkgd,cnkd->ctkgn", queries, key_heads, preferred_element_type=jnp.float32
    ) * HD ** (-0.5)
    scores = jnp.where(visible, scores, NEGATIVE)
    peak_new = jnp.maximum(peak_old, jnp.max(scores, axis=-1))
    weights = jnp.where(visible, jnp.exp(scores - peak_new[..., None]), 0.0)
    factor = jnp.exp(peak_old - peak_new)
    sum_new = sum_old * factor + jnp.sum(weights, axis=-1)
    acc_new = acc_old * factor[..., None] + jnp.einsum(
        "ctkgn,cnkd->ctkgd", weights, value_heads, precision=lax.Precision.HIGHEST
    )
    return (peak_new, sum_new, acc_new)


def normalize(hidden, norm_gain):
    widened = hidden.astype(jnp.float32)
    factor = lax.rsqrt(jnp.mean(widened * widened, axis=-1, keepdims=True) + EPSILON)
    return (widened * factor * norm_gain).astype(jnp.bfloat16)


def shard_stats(normed, token_ids, head, vocab_offset):
    logits = jnp.dot(normed, head, preferred_element_type=jnp.float32)
    maximum = jnp.max(logits, axis=1)
    total_mass = jnp.sum(jnp.exp(logits - maximum[:, None]), axis=1)
    columns = vocab_offset + jnp.arange(head.shape[1], dtype=jnp.int32)
    picked = jnp.sum(jnp.where(token_ids[:, None] == columns[None, :], logits, 0.0), axis=1)
    return (maximum, total_mass, picked)


def join_stats(first, second):
    maximum = jnp.maximum(first[0], second[0])
    total_mass = first[1] * jnp.exp(first[0] - maximum) + second[1] * jnp.exp(second[0] - maximum)
    return (maximum, total_mass, first[2] + second[2])


def per_device(
    cont_query,
    cont_key,
    cont_value,
    prefix_key,
    prefix_value,
    out_weight,
    norm_gain,
    lm_head,
    target_ids,
    cont_len,
    prompt_len,
    group_of,
    rewards,
):
    cont_count, cont_span, query_width = cont_query.shape
    own_rows = cont_count * cont_span
    kv_width = cont_key.shape[2]
    kv_heads = kv_width // HD
    per_group = query_width // kv_width
    device_index = lax.axis_index(SEQ)
    own_groups = lax.dynamic_slice_in_dim(group_of, device_index * cont_count, cont_count)
    own_prompt_len = prompt_len[own_groups]
    queries = cont_query.reshape(cont_count, cont_span, kv_heads, per_group, HD)
    shape_stats = (cont_count, cont_span, kv_heads, per_group)
    running = (
        jnp.full(shape_stats, NEGATIVE, jnp.float32),
        jnp.zeros(shape_stats, jnp.float32),
        jnp.zeros(shape_stats + (HD,), jnp.float32),
    )
    position = jnp.arange(cont_span, dtype=jnp.int32)
    causal = (position[None, :] <= position[:, None]).reshape(1, cont_span, 1, 1, cont_span)
    running = absorb(running, queries, cont_key, cont_value, causal)
    pieces = sent_together((prefix_key, prefix_value), SEQ, 1, 0)
    key_piece = jnp.take(pieces[0], own_groups, axis=0)
    value_piece = jnp.take(pieces[1], own_groups, axis=0)
    length = key_piece.shape[1]
    visible = jnp.arange(length, dtype=jnp.int32)[None, :] < own_prompt_len[:, None]
    running = absorb(
        running, queries, key_piece, value_piece, visible.reshape(cont_count, 1, 1, 1, length)
    )
    attended = (
        (running[2] / running[1][..., None]).astype(jnp.bfloat16).reshape(own_rows, query_width)
    )
    hidden_cols = jnp.dot(
        lax.all_gather(attended, SEQ, axis=0, tiled=True),
        out_weight,
        preferred_element_type=jnp.float32,
    ).astype(jnp.bfloat16)
    every_id = lax.all_gather(target_ids.reshape(own_rows), SEQ, axis=0, tiled=True)
    vocab_dev = lm_head.shape[1]
    vocab_offset = device_index * vocab_dev
    whole = lax.all_gather(hidden_cols, SEQ, axis=1, tiled=True)
    maximum, total_mass, picked = shard_stats(
        normalize(whole, norm_gain), every_id, lm_head, vocab_offset
    )
    merged = joined_all((maximum, total_mass, picked), SEQ, join_stats)
    maximum = lax.dynamic_slice_in_dim(merged[0], device_index * own_rows, own_rows)
    total_mass = lax.dynamic_slice_in_dim(merged[1], device_index * own_rows, own_rows)
    picked = lax.dynamic_slice_in_dim(merged[2], device_index * own_rows, own_rows)
    logprob = (picked - maximum - jnp.log(total_mass)).reshape(cont_count, cont_span)
    live = position[None, :] < cont_len[:, None]
    token_logprob = jnp.where(live, logprob, 0.0)
    every_reward = lax.all_gather(rewards, SEQ, axis=0, tiled=True)
    own_rows_groups = (own_groups[:, None] == group_of[None, :]).astype(jnp.float32)
    group_mean = jnp.dot(own_rows_groups, every_reward, precision=lax.Precision.HIGHEST) / GROUP
    deviation = every_reward[None, :] - group_mean[:, None]
    spread = jnp.sqrt(jnp.sum(own_rows_groups * deviation * deviation, axis=1) / (GROUP - 1))
    advantage = (rewards - group_mean) / jnp.maximum(spread, REWARD_FLOOR)
    objective = advantage * jnp.sum(token_logprob, axis=1) / cont_len.astype(jnp.float32)
    return (token_logprob, advantage, objective)


def solution(mesh):
    torus = Mesh(mesh.devices.reshape(mesh.shape["grp"], 16, 2), ("grp", "seq_0", "seq_1"))
    in_specs = (
        P(GRP_SEQ, None, None),
        P(GRP_SEQ, None, None),
        P(GRP_SEQ, None, None),
        P("grp", SEQ, None),
        P("grp", SEQ, None),
        P(None, SEQ),
        P(),
        P(None, SEQ),
        P(GRP_SEQ, None),
        P(GRP_SEQ),
        P("grp"),
        P("grp"),
        P(GRP_SEQ),
    )
    out_specs = (P(GRP_SEQ, None), P(GRP_SEQ), P(GRP_SEQ))
    return jax.shard_map(
        per_device, mesh=torus, in_specs=in_specs, out_specs=out_specs, check_vma=False
    )
```

profile of v0, /device:TPU:69, one launch (start us, length us, event | category | flops | bytes accessed | tf_op | source)
XLA Modules:
  0.0 438.0 jit_solution(7331179224173960218)
XLA Ops:
  7.2 0.0 copy-start
  7.2 0.1 all-gather.8.cloned.1.call-start
  7.3 1.9 pad_maximum_fusion
  9.2 0.1 all-gather.8.cloned.1.call-update
  9.2 0.1 all-gather.10.cloned.1.call-start
  9.3 1.4 reshape.1150
  10.7 0.0 copy-start.3
  10.7 0.9 reshape.1149
  11.6 0.9 reshape.1151
  12.5 0.7 compare_and_fusion
  13.2 1.3 gather_fusion
  14.6 0.6 fusion.124
  15.1 0.1 iota_compare_fusion
  15.2 104.9 %all-gather.8.cloned.1.call-done = bf16[8,2048,512]{2,1,0:T(8,128)(2,1)} async-done(((bf16[8,64,512]{2,1,0:T(8,128)(2,1)}), bf16[8,2048,512]{2,1,0:T(8,128)(2,1)}) %all-gather.8.cloned.1.call-update) | async-done | bytes 16777232 | tf_op jit(solution)/shard_map/all_gather | solution.py:21
  120.1 12.3 %fusion.122 = (bf16[4,1024,512]{2,1,0:T(8,128)(2,1)}, bf16[4,1024,512]{2,1,0:T(8,128)(2,1)}, bf16[4,1024,512]{2,1,0:T(8,128)(2,1)}, bf16[4,1024,512]{2,1,0:T(8,128)(2,1)}) fusion(bf16[8,2048,512]{2,1,0:T(8,128)(2,1)} %all-gather.8.cloned.1.call-done), kind=kLoop, calls=%fused_computation.204 | loop fusion | bytes 33554432 | tf_op jit(solution)/shard_map/jit(_take)/gather | solution.py:127
  132.4 0.0 copy-done.3
  132.4 2.9 gather_fusion.1
  135.3 4.3 gather_fusion.2
  139.5 4.2 gather_fusion.3
  143.7 4.2 gather_fusion.4
  147.9 6.3 %maximum_select_fusion.1 = (bf16[2,2048,512]{2,1,0:T(8,128)(2,1)}, bf16[2,2048,512]{2,1,0:T(8,128)(2,1)}) fusion(bf16[2,1024,512]{2,1,0:T(8,128)(2,1)} %gather_fusion.4, bf16[2,1024,512]{2,1,0:T(8,128)(2,1)} %gather_fusion.3, pred[2]{0:T(512)(128)(4,1)S(1)} %get-tuple-element.14, bf16[2,1024,512]{2,1,0:T(8,128)(2,1)} %gather_fusion.2, ...), kind=kLoop, calls=%fused_computation.29 | loop fusion | flops 20971520 | bytes 16777218 | tf_op jit(solution)/shard_map/jit(_take)/select_n | solution.py:127
  154.2 7.0 %reshape.1152 = bf16[2,2048,4,128]{3,2,1,0:T(4,128)(2,1)} reshape(bf16[2,2048,512]{2,1,0:T(8,128)(2,1)} %get-tuple-element.30) | data formatting | bytes 8388608 | tf_op jit(solution)/shard_map/reshape | solution.py:55
  161.2 6.9 %reshape.1153 = bf16[2,2048,4,128]{3,2,1,0:T(4,128)(2,1)} reshape(bf16[2,2048,512]{2,1,0:T(8,128)(2,1)} %get-tuple-element.29) | data formatting | bytes 8388608 | tf_op jit(solution)/shard_map/reshape | solution.py:56
  168.2 0.0 copy-done.4
  168.2 5.1 %bitcast_reduce_fusion = (f32[2,32,4,5]{1,3,2,0:T(8,128)S(1)}, f32[2,4,2048,32,5]{2,3,4,1,0:T(8,128)S(1)}) fusion(pred[2,2048]{1,0:T(4,128)(4,1)S(1)} %iota_compare_fusion, bf16[2,32,4,5,128]{4,3,2,1,0:T(8,128)(2,1)S(1)} %copy-done.4, bf16[2,2048,4,128,1]{3,2,1,0,4:T(4,128)(2,1)} %bitcast.390), kind=kOutput, calls=%fused_computation.14 | convolution fusion | flops 678951680 | bytes 15016960 | tf_op jit(solution)/shard_map/ctkgd,cnkd->ctkgn/dot_general | solution.py:57
  173.2 0.0 copy-start.2
  173.3 2.8 fusion.9
  176.1 7.1 %fusion.21 = f32[2,32,4,5,128]{4,1,3,2,0:T(8,128)S(1)} fusion(f32[2,4,2048,32,5]{2,3,4,1,0:T(8,128)S(1)} %get-tuple-element.34, f32[2,32,4,5]{1,3,2,0:T(8,128)S(1)} %get-tuple-element.27, pred[2,2048]{1,0:T(4,128)(4,1)S(1)} %iota_compare_fusion, bf16[2,2048,4,128,1]{3,2,1,0,4:T(4,128)(2,1)S(1)} %bitcast.389), kind=kOutput, calls=%fused_computation.34 | convolution fusion | flops 4037017600 | bytes 15344640 | tf_op jit(solution)/shard_map/ctkgn,cnkd->ctkgd/dot_general | solution.py:65
  183.2 0.2 fusion.34
  183.4 1.3 fusion.32
  184.7 0.0 copy-start.9
  184.8 0.0 copy-start.10
  184.8 0.0 copy-start.7
  184.8 0.0 copy-start.5
  184.8 0.2 copy.46
  185.0 1.1 reshape.1154
  186.1 0.1 all-gather.10.cloned.1.call-update
  186.1 0.3 all-gather.12.cloned.1.call-start
  186.4 75.9 %all-gather.10.cloned.1.call-done = bf16[2048,2560]{1,0:T(8,128)(2,1)} async-done(((bf16[64,2560]{1,0:T(8,128)(2,1)}), bf16[2048,2560]{1,0:T(8,128)(2,1)}) %all-gather.10.cloned.1.call-update) | async-done | bytes 10485776 | tf_op jit(solution)/shard_map/all_gather | solution.py:137
  262.4 0.0 copy-done
  262.4 8.0 %convolution_convert_fusion = bf16[2048,80]{0,1:T(8,128)(2,1)} fusion(bf16[2048,2560]{1,0:T(8,128)(2,1)} %all-gather.10.cloned.1.call-done, bf16[2560,80]{0,1:T(8,128)(2,1)S(1)} %copy-done), kind=kOutput, calls=%fused_computation.33 | convolution fusion | flops 839024640 | bytes 11223040 | tf_op jit(solution)/shard_map/dot_general | solution.py:136
  270.4 0.1 all-gather.12.cloned.1.call-update
  270.4 0.1 reshape.1215
  270.5 0.0 copy-done.10
  270.5 0.6 dynamic-slice.1
  272.4 0.3 dynamic-update-slice
  272.7 0.2 dynamic-update-slice.1
  272.9 47.3 %all-reduce.1 = f32[64]{0:T(128)S(1)} all-reduce(f32[64]{0:T(128)S(1)} %dynamic-update-slice.1), channel_id=1, replica_groups=mesh['grp'=4,'seq_0'=16,'seq_1'=2] {'seq_0','seq_1'}, use_global_device_ids=true, to_apply=%add.1 | all-reduce | flops 64 | bytes 512
  320.2 18.7 %all-reduce = s32[2048]{0:T(1024)S(1)} all-reduce(s32[2048]{0:T(1024)S(1)} %dynamic-update-slice), channel_id=1, replica_groups=mesh['grp'=4,'seq_0'=16,'seq_1'=2] {'seq_0','seq_1'}, use_global_device_ids=true, to_apply=%add | all-reduce | flops 2048 | bytes 16384
  339.0 0.2 fusion.33
  339.2 0.2 fusion.105
  339.4 6.2 %all-gather.12.cloned.1.call-done = bf16[2048,2560]{0,1:T(8,128)(2,1)} async-done(((bf16[2048,80]{0,1:T(8,128)(2,1)}), bf16[2048,2560]{0,1:T(8,128)(2,1)}) %all-gather.12.cloned.1.call-update) | async-done | bytes 10485776 | tf_op jit(solution)/shard_map/all_gather | solution.py:144
  345.5 6.1 %fusion = f32[2048]{0:T(1024)S(1)} fusion(bf16[2048,2560]{0,1:T(8,128)(2,1)} %all-gather.12.cloned.1.call-done), kind=kLoop, calls=%fused_computation.7 | loop fusion | flops 15726592 | bytes 10493952 | tf_op jit(solution)/shard_map/reduce_sum | solution.py:73
  351.7 35.2 %fusion.125 = (f32[2048]{0:T(1024)S(1)}, f32[2048,2376]{0,1:T(8,128)}) fusion(bf16[2560,2376]{0,1:T(8,128)(2,1)} %param.22, bf16[2048,2560]{0,1:T(8,128)(2,1)} %all-gather.12.cloned.1.call-done, f32[2560]{0:T(1024)S(1)} %copy-done.8, f32[2048]{0:T(1024)S(1)} %add_rsqrt_fusion), kind=kOutput, calls=%fused_computation.207 | convolution fusion | flops 24940001280 | bytes 42141696 | tf_op jit(solution)/shard_map/dot_general | solution.py:78
  386.8 9.7 %exponential_reduce_fusion = (f32[2048]{0:T(1024)S(1)}, f32[2048]{0:T(1024)S(1)}) fusion(f32[2048,2376]{0,1:T(8,128)} %get-tuple-element.36, f32[2048]{0:T(1024)S(1)} %get-tuple-element.35, s32[2376]{0:T(1024)S(1)} %iota_add_fusion, s32[2048]{0:T(1024)S(1)} %all-reduce), kind=kLoop, calls=%fused_computation.11 | loop fusion | flops 24326144 | bytes 19506464 | tf_op jit(solution)/shard_map/reduce_sum | solution.py:80
  396.6 24.1 %all-gather.2 = f32[16,3,2048]{2,1,0:T(4,128)S(1)} all-gather(f32[1,3,2048]{2,1,0:T(4,128)S(1)} %maximum_bitcast_fusion), channel_id=2, replica_groups=mesh['grp'=4,'seq_0'=16,'seq_1'=2] {'seq_0'}, dimensions={0}, use_global_device_ids=true | all-gather | bytes 417792 | tf_op jit(solution)/shard_map/all_gather | solution.py:33
  420.8 0.4 fusion.44
  421.2 0.1 fusion.42
  421.3 8.6 %all-gather.3 = f32[2,3,2048]{2,1,0:T(4,128)S(1)} all-gather(f32[1,3,2048]{2,1,0:T(4,128)S(1)} %maximum_bitcast_fusion.1), channel_id=3, replica_groups=mesh['grp'=4,'seq_0'=16,'seq_1'=2] {'seq_1'}, dimensions={0}, use_global_device_ids=true | all-gather | bytes 73728 | tf_op jit(solution)/shard_map/all_gather | solution.py:33
  430.0 0.1 fusion.111
  430.1 0.1 reshape.1159
  430.1 0.8 fusion.120
  430.9 0.5 convert_divide_fusion
  431.4 0.0 copy-done.1
  (23 shorter events, 0.2 us)
Async XLA Ops:
  7.2 255.2 %copy-start = (bf16[2560,80]{0,1:T(8,128)(2,1)S(1)}, bf16[2560,80]{0,1:T(8,128)(2,1)}, u32[]{:S(2)}) copy-start(bf16[2560,80]{0,1:T(8,128)(2,1)} %param.20) | copy-start | bytes 1228804
  7.2 113.0 %all-gather.8.cloned.1.call-start = ((), (), s32[]{:S(2)}) async-start(), calls=%async_computation | async-start | bytes 17301504 | tf_op jit(solution)/shard_map/all_gather | solution.py:21
  9.2 253.1 %all-gather.10.cloned.1.call-start = ((), (), s32[]{:S(2)}) async-start(), calls=%async_computation.1 | async-start | bytes 10813440 | tf_op jit(solution)/shard_map/all_gather | solution.py:137
  10.7 121.7 %copy-start.3 = (bf16[2,32,4,5,128]{4,3,2,1,0:T(8,128)(2,1)}, bf16[2,32,4,5,128]{4,3,2,1,0:T(8,128)(2,1)S(1)}, u32[]{:S(2)}) copy-start(bf16[2,32,4,5,128]{4,3,2,1,0:T(8,128)(2,1)S(1)} %reshape.1150) | copy-start | bytes 983044
  154.2 13.9 %copy-start.4 = (bf16[2,32,4,5,128]{4,3,2,1,0:T(8,128)(2,1)S(1)}, bf16[2,32,4,5,128]{4,3,2,1,0:T(8,128)(2,1)}, u32[]{:S(2)}) copy-start(bf16[2,32,4,5,128]{4,3,2,1,0:T(8,128)(2,1)} %copy-done.3) | copy-start | bytes 983044
  173.2 2.9 copy-start.2
  184.7 85.7 %copy-start.9 = (s32[2,32]{1,0:T(2,128)S(1)}, s32[2,32]{1,0:T(2,128)}, u32[]{:S(2)}) copy-start(s32[2,32]{1,0:T(2,128)} %param.23) | copy-start | bytes 772
  184.8 85.8 %copy-start.10 = (u32[128]{0:T(128)S(1)}, u32[128]{0:T(128)}, u32[]{:S(2)}) copy-start(u32[128]{0:T(128)} %constant.68) | copy-start | bytes 1540
  184.8 87.9 %copy-start.7 = (f32[2]{0:T(128)S(1)}, f32[2]{0:T(128)}, u32[]{:S(2)}) copy-start(f32[2]{0:T(128)} %param.27) | copy-start | bytes 28
  184.8 154.2 %copy-start.5 = (s32[64]{0:T(128)S(1)}, s32[64]{0:T(128)}, u32[]{:S(2)}) copy-start(s32[64]{0:T(128)} %param.26) | copy-start | bytes 772
  186.1 159.4 %all-gather.12.cloned.1.call-start = ((), (), s32[]{:S(2)}) async-start(), calls=%async_computation.2 | async-start | bytes 10813440 | tf_op jit(solution)/shard_map/all_gather | solution.py:144
  270.4 81.3 %copy-start.8 = (f32[2560]{0:T(1024)S(1)}, f32[2560]{0:T(1024)}, u32[]{:S(2)}) copy-start(f32[2560]{0:T(1024)} %param.21) | copy-start | bytes 30724
  386.8 44.6 %copy-start.1 = (bf16[2560,80]{0,1:T(8,128)(2,1)S(1)}, bf16[2560,80]{0,1:T(8,128)(2,1)}, u32[]{:S(2)}) copy-start(bf16[2560,80]{0,1:T(8,128)(2,1)} %param.20) | copy-start | bytes 1228804
  386.8 43.3 %copy-start.6 = (s32[2]{0:T(128)S(1)}, s32[2]{0:T(128)}, u32[]{:S(2)}) copy-start(s32[2]{0:T(128)} %param.24) | copy-start | bytes 28
Sparse Core Ops, SparseCore 0:
  9.8 110.3 all-gather.7
  186.3 76.0 all-gather.9
  270.5 74.9 all-gather.11
where the time goes:
time: 439 us; the launch traced here: 438 us
  waiting for transfers between devices  187 us (43%)
  blocking collectives  98.8 us (23%)
  matrix products  57.4 us (13%)
  local copies, waits for them, and re-layouts  48.8 us (11%)
  other arithmetic  30.1 us (7%)
  between operations  15.3 us (3%)
    all_gather x1, waiting for transfers between devices, sent_together(): whole = lax.all_gather(both, axis, axis=dim, tiled=True)  105 us
    all_gather x1, waiting for transfers between devices, per_device(): lax.all_gather(attended, SEQ, axis=0, tiled=True)  75.9 us
    unnamed x2, blocking collectives  66 us
    dot_general x1, matrix products, shard_stats(): logits = jnp.dot(normed, head, preferred_element_type=jnp.float32)  35.2 us
    all_gather x2, blocking collectives, gathered_once(): both, at, found = (lax.all_gather(jnp.concatenate(lines), axis), 0, {})  32.7 us
    gather x3, local copies, waits for them, and re-layouts, per_device(): value_piece = jnp.take(pieces[1], own_groups, axis=0)  20.6 us
    reduce_sum x1, other arithmetic, shard_stats(): total_mass = jnp.sum(jnp.exp(logits - maximum[:, None]), axis=1)  9.72 us
  transfers between devices with their start and end apart: 3, of which 3 were waited for; matrix products, arithmetic and copies ran while one was open for 2% of the time, Pallas kernels for 0%

commit v1 on v0

v1 whole, which is shorter than its diff:
```python
import functools

import jax
import jax.numpy as jnp
from jax import lax
from jax.experimental import pallas as pl
from jax.experimental.pallas import tpu as pltpu
from jax.sharding import PartitionSpec as P

HD = 128
GROUP = 16
NEGATIVE = -1e30
EPSILON = 1e-06
REWARD_FLOOR = 0.25

CORES = 2
CHUNKS = 4
SKEW = 3
TILE = 480
HALF = 8

BF16 = jnp.bfloat16
F32 = jnp.float32


def dot_last(a, b):
    return lax.dot_general(a, b, (((1,), (1,)), ((), ())), preferred_element_type=F32)


def send(src, dst, send_sem, recv_sem, device):
    return pltpu.make_async_remote_copy(
        src_ref=src,
        dst_ref=dst,
        send_sem=send_sem,
        recv_sem=recv_sem,
        device_id={"seq": device},
        device_id_type=pl.DeviceIdType.MESH,
    )


def kernel(
    dims,
    group_of,
    prompt_len,
    small,
    q,
    ck,
    cv,
    pk,
    pv,
    wt,
    gain,
    lm,
    out,
    kvs,
    kvr,
    qs,
    qr,
    ab,
    hb,
    nt,
    wv,
    gv,
    lv,
    smv,
    smg,
    run_m,
    run_s,
    run_p,
    st,
    sr,
    loc,
    kv_rs,
    kv_rd,
    kv_so,
    kv_sd,
    kv_su,
    kv_sn,
    q_rs,
    q_ss,
    sm_rs,
    sm_ss,
    g_rs,
    g_rd,
    g_sr,
    g_sl,
    g_sd,
    st_rs,
    st_ss,
):
    n, heads, per_head, conts, span, positions = dims
    chips = n // CORES
    side = chips // heads
    vocab = lm.shape[0]
    rows_q = conts * per_head * span
    one_q = per_head * span
    own = conts * span
    feats = wt.shape[0]
    width = per_head * HD
    chunk_rows = n // CHUNKS * own

    me = lax.axis_index("seq")
    z = lax.div(me, CORES)
    co = lax.rem(me, CORES)
    partner = me + 1 - 2 * co
    k0 = lax.div(z, side)
    j = lax.rem(z, side)
    base = k0 * side

    def chip(at):
        return lax.rem(at + chips, chips)

    def dev(at):
        return chip(at) * CORES + co

    def kv_loads(head):
        lanes = pl.ds(pl.multiple_of(head * HD, HD), HD)
        return lanes

    def load_kv(head, carry):
        lanes = kv_loads(head)
        pltpu.make_async_copy(pk.at[:, :, lanes], kvs.at[head, 0], loc.at[0]).start()
        pltpu.make_async_copy(pv.at[:, :, lanes], kvs.at[head, 1], loc.at[0]).start()
        return carry

    lax.fori_loop(0, heads, load_kv, 0)

    def load_q(head, carry):
        for a in range(conts):
            for g in range(per_head):
                lanes = pl.ds(pl.multiple_of((head * per_head + g) * HD, HD), HD)
                pltpu.make_async_copy(
                    q.at[a, :, lanes], qs.at[head, pl.ds(a * one_q + g * span, span), :], loc.at[1]
                ).start()
            lanes = pl.ds(pl.multiple_of(head * HD, HD), HD)
            pltpu.make_async_copy(
                ck.at[a, :, lanes], qs.at[head, pl.ds(rows_q + a * span, span), :], loc.at[1]
            ).start()
            pltpu.make_async_copy(
                cv.at[a, :, lanes], qs.at[head, pl.ds(rows_q + own + a * span, span), :], loc.at[1]
            ).start()
        return carry

    lax.fori_loop(0, heads, load_q, 0)
    pltpu.make_async_copy(small, smv, loc.at[2]).start()

    barrier = pltpu.get_barrier_semaphore()

    def greet(d, carry):
        @pl.when(d != me)
        def _():
            pl.semaphore_signal(
                barrier, inc=1, device_id={"seq": d}, device_id_type=pl.DeviceIdType.MESH
            )

        return carry

    lax.fori_loop(0, n, greet, 0)
    pltpu.make_async_copy(kvs, kvs, loc.at[0]).wait()
    pl.semaphore_wait(barrier, n - 1)

    def kv_at(src):
        rows = pl.ds(pl.multiple_of((chip(src) * CORES + co) * positions, positions), positions)
        return kvr.at[:, :, rows, :]

    def kv_sem(src):
        return chip(src)

    def kv_send(source, head_block, target, send_sem):
        return send(head_block, kv_at(source), send_sem, kv_rs.at[kv_sem(source)], dev(target))

    def kv_d2d(source, block):
        return send(
            block, kv_at(source), kv_sd.at[kv_sem(source)], kv_rd.at[kv_sem(source)], partner
        )

    next_head = lax.rem(k0 + 1, heads)
    prev_head = lax.rem(k0 + heads - 1, heads)
    far_head = lax.rem(k0 + 2, heads)
    own_right = kv_send(z, kvs.at[k0], z + 1, kv_so.at[0])
    own_left = kv_send(z, kvs.at[k0], z - 1, kv_so.at[1])
    ext_right = kv_send(z, kvs.at[next_head], base + side, kv_so.at[2])
    ext_left = kv_send(z, kvs.at[prev_head], base - 1, kv_so.at[3])
    far_right = kv_send(z, kvs.at[far_head], base + 2 * side, kv_so.at[4])
    far_left = kv_send(z, kvs.at[far_head], base - side - 1, kv_so.at[5])
    own_part = kv_d2d(z, kvs.at[k0])

    @pl.when(j >= side // 2)
    def _():
        far_right.start()

    @pl.when(j < side // 2)
    def _():
        far_left.start()

    ext_right.start()
    ext_left.start()

    @pl.when(j < side - 1)
    def _():
        own_right.start()

    @pl.when(j > 0)
    def _():
        own_left.start()

    own_part.start()
    own_rows = pl.ds(pl.multiple_of(me * positions, positions), positions)
    own_lanes = pl.ds(pl.multiple_of(k0 * HD, HD), HD)
    keep_k = pltpu.make_async_copy(pk.at[:, :, own_lanes], kvr.at[0, :, own_rows, :], loc.at[3])
    keep_v = pltpu.make_async_copy(pv.at[:, :, own_lanes], kvr.at[1, :, own_rows, :], loc.at[4])
    keep_k.start()
    keep_v.start()

    pltpu.make_async_copy(qs, qs, loc.at[1]).wait()

    def q_send(step):
        target = chip(z + side * step)
        return send(
            qs.at[lax.div(target, side)],
            qr.at[k0],
            q_ss.at[step],
            q_rs.at[k0],
            dev(target),
        )

    for step in range(1, heads):
        q_send(step).start()

    keep_q = []
    for a in range(conts):
        for g in range(per_head):
            lanes = pl.ds(pl.multiple_of((k0 * per_head + g) * HD, HD), HD)
            keep_q.append((q.at[a, :, lanes], pl.ds(a * one_q + g * span, span)))
        keep_q.append((ck.at[a, :, own_lanes], pl.ds(rows_q + a * span, span)))
        keep_q.append((cv.at[a, :, own_lanes], pl.ds(rows_q + own + a * span, span)))
    for source, rows in keep_q:
        pltpu.make_async_copy(source, qr.at[k0, rows, :], loc.at[5]).start()

    pltpu.make_async_copy(small, smv, loc.at[2]).wait()

    def small_send(d):
        return send(smv, smg.at[me], sm_ss.at[d], sm_rs.at[me], d)

    def small_out(d, carry):
        @pl.when(d != me)
        def _():
            small_send(d).start()

        return carry

    lax.fori_loop(0, n, small_out, 0)
    keep_small = pltpu.make_async_copy(small, smg.at[me], loc.at[2])
    keep_small.start()
    load_w = pltpu.make_async_copy(wt, wv, loc.at[6])
    load_w.start()
    load_gain = pltpu.make_async_copy(gain, gv, loc.at[7])
    load_gain.start()
    load_lm = pltpu.make_async_copy(lm, lv.at[pl.ds(0, vocab), :], loc.at[8])
    load_lm.start()

    reach = side + side // 2

    def up_send(t):
        return kv_send(z - t, kv_at(z - t), z + 1, kv_su.at[t - 1])

    def down_send(t):
        return kv_send(z + t, kv_at(z + t), z - 1, kv_sn.at[t - 1])

    def chain(i, carry):
        t = i + 1

        @pl.when(t <= j + reach)
        def _():
            kv_send(z - t, kv_at(z - t), z + 1, kv_su.at[t - 1]).wait_recv()

            @pl.when(j < side - 1)
            def _():
                up_send(t).start()

            kv_d2d(z - t, kv_at(z - t)).start()

        @pl.when(t <= side - 1 - j + reach)
        def _():
            kv_send(z + t, kv_at(z + t), z - 1, kv_sn.at[t - 1]).wait_recv()

            @pl.when(j > 0)
            def _():
                down_send(t).start()

            kv_d2d(z + t, kv_at(z + t)).start()

        return carry

    longest = side - 1 + reach
    lax.fori_loop(0, longest, chain, 0)

    keep_k.wait()
    keep_v.wait()
    pltpu.make_async_copy(qr.at[k0], qr.at[k0], loc.at[5]).wait()

    def other_rows(src):
        rows = pl.ds(
            pl.multiple_of((src * CORES + 1 - co) * positions, positions), positions
        )
        return kvr.at[:, :, rows, :]

    def kv_partner(src, carry):
        send(other_rows(src), other_rows(src), kv_sd.at[src], kv_rd.at[src], partner).wait_recv()
        return carry

    lax.fori_loop(0, chips, kv_partner, 0)

    def q_arrived(c, carry):
        @pl.when(c != k0)
        def _():
            send(qr.at[c], qr.at[c], q_ss.at[0], q_rs.at[c], partner).wait_recv()

        return carry

    lax.fori_loop(0, heads, q_arrived, 0)

    def block_at(stream, chip_id, core):
        d = chip(chip_id) * CORES + core
        if stream < CHUNKS:
            return ab.at[stream, pl.ds(pl.multiple_of(d * own, own), own), :]
        return hb.at[stream - CHUNKS, pl.ds(pl.multiple_of(d * feats, 16), feats), :]

    def ring_send(stream, source, target, send_sem):
        block = block_at(stream, source, co)
        return send(block, block, send_sem, g_rs.at[stream, chip(source)], dev(target))

    def ring_right(stream, t):
        return ring_send(stream, z - t, z + 1, g_sr.at[stream, t])

    def ring_left(stream, t):
        return ring_send(stream, z + t, z - 1, g_sl.at[stream, t])

    def ring_d2d(stream, source):
        block = block_at(stream, source, co)
        return send(
            block, block, g_sd.at[stream, chip(source)], g_rd.at[stream, chip(source)], partner
        )

    def steps_of(stream):
        right = HALF if stream % 2 == 0 else chips - 1 - HALF
        return right, chips - 1 - right

    def ring_open(stream):
        ring_right(stream, 0).start()
        ring_left(stream, 0).start()
        ring_d2d(stream, z).start()

    def ring_step(stream, t):
        right, left = steps_of(stream)

        @pl.when(t <= right)
        def _():
            ring_send(stream, z - t, z + 1, g_sr.at[stream, 0]).wait_recv()

            @pl.when(t < right)
            def _():
                ring_right(stream, t).start()

        @pl.when(t <= left)
        def _():
            ring_send(stream, z + t, z - 1, g_sl.at[stream, 0]).wait_recv()

            @pl.when(t < left)
            def _():
                ring_left(stream, t).start()

        @pl.when(t <= right)
        def _():
            ring_d2d(stream, z - t).start()

        @pl.when(t <= left)
        def _():
            ring_d2d(stream, z + t).start()

    def ring_partner(stream):
        def arrived(src, carry):
            block = block_at(stream, src, 1 - co)
            send(
                block, block, g_sd.at[stream, src], g_rd.at[stream, src], partner
            ).wait_recv()
            return carry

        lax.fori_loop(0, chips, arrived, 0)

    def attention(c):
        for a in range(conts):
            cont = ((c * side + j) * CORES + co) * conts + a
            g = group_of[cont]
            length = prompt_len[g]
            queries = qr[c, pl.ds(a * one_q, one_q), :]
            own_keys = qr[c, pl.ds(rows_q + a * span, span), :]
            own_values = qr[c, pl.ds(rows_q + own + a * span, span), :]
            scores = dot_last(queries, kvr[0, g]) * HD ** (-0.5)
            at = lax.broadcasted_iota(jnp.int32, scores.shape, 1)
            scores = jnp.where(at < length, scores, NEGATIVE)
            near = dot_last(queries, own_keys) * HD ** (-0.5)
            token = lax.rem(lax.broadcasted_iota(jnp.int32, near.shape, 0), span)
            near = jnp.where(lax.broadcasted_iota(jnp.int32, near.shape, 1) <= token, near, NEGATIVE)
            peak = jnp.maximum(
                jnp.max(scores, axis=1, keepdims=True), jnp.max(near, axis=1, keepdims=True)
            )
            weights = jnp.exp(scores - peak)
            near = jnp.exp(near - peak)
            total = jnp.sum(weights, axis=1, keepdims=True) + jnp.sum(near, axis=1, keepdims=True)
            mixed = jnp.dot(weights.astype(BF16), kvr[1, g], preferred_element_type=F32)
            mixed += jnp.dot(near.astype(BF16), own_values, preferred_element_type=F32)
            mixed = (mixed / total).astype(BF16)
            rows = pl.ds(pl.multiple_of(me * own + a * span, span), span)
            for g5 in range(per_head):
                ab[c, rows, g5 * HD : (g5 + 1) * HD] = mixed[g5 * span : (g5 + 1) * span, :]

    def project(c):
        total = jnp.zeros((feats, chunk_rows), F32)
        for k in range(heads):
            total += dot_last(
                wv[:, k * width : (k + 1) * width], ab[c, pl.ds(k * chunk_rows, chunk_rows), :]
            )
        hb[c, pl.ds(pl.multiple_of(me * feats, 16), feats), :] = total.astype(BF16)

    features = hb.shape[1]
    strip = HD

    def normalize(c):
        def squares(i, total):
            x = hb[c, pl.ds(pl.multiple_of(i * strip, strip), strip), :].astype(F32)
            return total + jnp.sum(x * x, axis=0, keepdims=True)

        total = lax.fori_loop(0, features // strip, squares, jnp.zeros((1, chunk_rows), F32))
        factor = lax.rsqrt(total / features + EPSILON)

        def scale(i, carry):
            rows = pl.ds(pl.multiple_of(i * strip, strip), strip)
            nt[rows, :] = (hb[c, rows, :].astype(F32) * factor * gv[rows, :]).astype(BF16)
            return carry

        lax.fori_loop(0, features // strip, scale, 0)

    def chunk_ids(c):
        rows = []
        for i in range(side):
            d = (c * side + i) * CORES
            rows.append(smg[d, 0:1, :] + smg[d + 1, 0:1, :])
        ids = jnp.concatenate(rows, axis=1).astype(jnp.int32) - me * vocab
        return jnp.where(ids < vocab, ids, -1)

    def tile(c, v):
        rows = pl.ds(pl.multiple_of(v * TILE, 16), TILE)
        logits = jnp.dot(lv[rows, :], nt[...], preferred_element_type=F32)
        at = lax.broadcasted_iota(jnp.int32, logits.shape, 0) + v * TILE
        logits = jnp.where(at < vocab, logits, NEGATIVE)
        run_p[...] += jnp.sum(jnp.where(at == chunk_ids(c), logits, 0.0), axis=0, keepdims=True)
        old = run_m[...]
        new = jnp.maximum(old, jnp.max(logits, axis=0, keepdims=True))
        run_s[...] = run_s[...] * jnp.exp(old - new) + jnp.sum(
            jnp.exp(logits - new), axis=0, keepdims=True
        )
        run_m[...] = new

    def stats_send(c, i, core):
        d = (c * side + i) * CORES + core
        return d, send(st.at[c, i], sr.at[me], st_ss.at[d], st_rs.at[me], d)

    def stats_out(c):
        lse = run_m[...] + jnp.log(run_s[...])
        hit = run_p[...]
        for i in range(side):
            lanes = slice(i * HD, (i + 1) * HD)
            st[c, i, 0:1, :] = lse[:, lanes]
            st[c, i, 1:2, :] = hit[:, lanes]

        @pl.when(k0 == c)
        def _():
            own_lse, own_hit = lse[:, 0:HD], hit[:, 0:HD]
            for i in range(1, side):
                lanes = slice(i * HD, (i + 1) * HD)
                own_lse = jnp.where(j == i, lse[:, lanes], own_lse)
                own_hit = jnp.where(j == i, hit[:, lanes], own_hit)
            sr[me, 0:1, :] = own_lse
            sr[me, 1:2, :] = own_hit

        for i in range(side):
            for core in range(CORES):
                d, copy = stats_send(c, i, core)

                @pl.when(d != me)
                def _(copy=copy):
                    copy.start()

    tiles = -(-vocab // TILE)
    per_slot = -(-(tiles - 1) // (SKEW - 1))

    def slot(i, carry):
        for stream in range(CHUNKS, 2 * CHUNKS):
            t = i - (SKEW * (stream - CHUNKS) + HALF)

            @pl.when(jnp.logical_and(t >= 1, t <= HALF))
            def _(stream=stream, t=t):
                ring_step(stream, t)

        for stream in range(CHUNKS):
            t = i - SKEW * stream

            @pl.when(jnp.logical_and(t >= 1, t <= HALF))
            def _(stream=stream, t=t):
                ring_step(stream, t)

        @pl.when(jnp.logical_and(lax.rem(i, SKEW) == 0, i < SKEW * CHUNKS))
        def _():
            attention(lax.div(i, SKEW))

        for c in range(CHUNKS):

            @pl.when(i == SKEW * c)
            def _(c=c):
                ring_open(c)

        @pl.when(i == HALF)
        def _():
            load_w.wait()

        for c in range(CHUNKS):

            @pl.when(i == SKEW * c + HALF)
            def _(c=c):
                ring_partner(c)
                project(c)
                ring_open(CHUNKS + c)

        m = i - 2 * HALF

        @pl.when(m == 0)
        def _():
            load_gain.wait()
            load_lm.wait()
            keep_small.wait()

            def small_in(d, carry):
                @pl.when(d != me)
                def _():
                    send(smg.at[d], smg.at[d], sm_ss.at[d], sm_rs.at[d], partner).wait_recv()

                return carry

            lax.fori_loop(0, n, small_in, 0)

        for c in range(CHUNKS):

            @pl.when(m == SKEW * c)
            def _(c=c):
                ring_partner(CHUNKS + c)

        @pl.when(m >= 0)
        def _():
            c = lax.div(m, SKEW)
            r = lax.rem(m, SKEW)

            @pl.when(r == 0)
            def _():
                normalize(c)
                run_m[...] = jnp.full_like(run_m, NEGATIVE)
                run_s[...] = jnp.zeros_like(run_s)
                run_p[...] = jnp.zeros_like(run_p)

            first = jnp.maximum(1 + (r - 1) * per_slot, 0)
            first = jnp.where(r == 0, 0, first)
            last = jnp.minimum(1 + r * per_slot, tiles)

            def one(v, carry):
                tile(c, v)
                return carry

            lax.fori_loop(first, last, one, 0)

        for c in range(CHUNKS):

            @pl.when(m == SKEW * c + SKEW - 1)
            def _(c=c):
                stats_out(c)

        return carry

    lax.fori_loop(0, 2 * HALF + SKEW * CHUNKS, slot, 0)

    def stats_in(d, carry):
        @pl.when(d != me)
        def _():
            send(sr.at[d], sr.at[d], st_ss.at[d], st_rs.at[d], partner).wait_recv()

        return carry

    lax.fori_loop(0, n, stats_in, 0)
    everyone = sr[...]
    lse = everyone[:, 0, :]
    peak = jnp.max(lse, axis=0, keepdims=True)
    lse = peak + jnp.log(jnp.sum(jnp.exp(lse - peak), axis=0, keepdims=True))
    out[0:1, :] = jnp.sum(everyone[:, 1, :], axis=0, keepdims=True) - lse
    out[1:2, :] = jnp.sum(smg[...][:, 1, :], axis=0, keepdims=True)

    @pl.when(j >= side // 2)
    def _():
        far_right.wait_send()

    @pl.when(j < side // 2)
    def _():
        far_left.wait_send()

    ext_right.wait_send()
    ext_left.wait_send()

    @pl.when(j < side - 1)
    def _():
        own_right.wait_send()

    @pl.when(j > 0)
    def _():
        own_left.wait_send()

    own_part.wait_send()
    for step in range(1, heads):
        q_send(step).wait_send()

    def chain_out(i, carry):
        t = i + 1

        @pl.when(t <= j + reach)
        def _():
            @pl.when(j < side - 1)
            def _():
                up_send(t).wait_send()

            kv_d2d(z - t, kv_at(z - t)).wait_send()

        @pl.when(t <= side - 1 - j + reach)
        def _():
            @pl.when(j > 0)
            def _():
                down_send(t).wait_send()

            kv_d2d(z + t, kv_at(z + t)).wait_send()

        return carry

    lax.fori_loop(0, longest, chain_out, 0)

    def peers_out(d, carry):
        @pl.when(d != me)
        def _():
            small_send(d).wait_send()
            send(st.at[0, 0], sr.at[me], st_ss.at[d], st_rs.at[me], d).wait_send()

        return carry

    lax.fori_loop(0, n, peers_out, 0)

    def ring_out(t, carry):
        for stream in range(2 * CHUNKS):
            right, left = steps_of(stream)

            @pl.when(t < right)
            def _(stream=stream):
                ring_right(stream, t).wait_send()

            @pl.when(t < left)
            def _(stream=stream):
                ring_left(stream, t).wait_send()

            ring_d2d(stream, t).wait_send()
            ring_d2d(stream, t + HALF).wait_send()
        return carry

    lax.fori_loop(0, HALF, ring_out, 0)


def scores_of(
    n, group_of, prompt_len, small, q, ck, cv, pk, pv, wt, gain, lm
):
    conts, span, query_width = q.shape
    prompts, positions, kv_width = pk.shape
    heads = kv_width // HD
    per_head = query_width // kv_width
    chips = n // CORES
    own = conts * span
    feats, features = wt.shape
    vocab = lm.shape[0]
    chunk_rows = n // CHUNKS * own
    chunk_q = own * per_head + 2 * own
    streams = 2 * CHUNKS
    side = chips // heads
    dims = (n, heads, per_head, conts, span, positions)
    dma = pltpu.SemaphoreType.DMA
    vmem_rows = -(-vocab // TILE) * TILE
    any_spec = pl.BlockSpec(memory_space=pl.ANY)
    smem_spec = pl.BlockSpec(memory_space=pltpu.SMEM)
    return pl.pallas_call(
        functools.partial(kernel, dims),
        out_shape=jax.ShapeDtypeStruct((2, HD), F32),
        in_specs=[smem_spec] * 2 + [any_spec] * 9,
        out_specs=pl.BlockSpec(memory_space=pltpu.VMEM),
        scratch_shapes=[
            pltpu.VMEM((heads, 2, prompts, positions, HD), BF16),
            pltpu.VMEM((2, prompts, n * positions, HD), BF16),
            pltpu.VMEM((heads, chunk_q, HD), BF16),
            pltpu.VMEM((heads, chunk_q, HD), BF16),
            pltpu.VMEM((CHUNKS, n * own, per_head * HD), BF16),
            pltpu.VMEM((CHUNKS, n * feats, chunk_rows), BF16),
            pltpu.VMEM((n * feats, chunk_rows), BF16),
            pltpu.VMEM((feats, features), BF16),
            pltpu.VMEM((n * feats, 1), F32),
            pltpu.VMEM((vmem_rows, n * feats), BF16),
            pltpu.VMEM((2, HD), F32),
            pltpu.VMEM((n, 2, HD), F32),
            pltpu.VMEM((1, chunk_rows), F32),
            pltpu.VMEM((1, chunk_rows), F32),
            pltpu.VMEM((1, chunk_rows), F32),
            pltpu.VMEM((CHUNKS, side, 2, HD), F32),
            pltpu.VMEM((n, 2, HD), F32),
            dma((9,)),
            dma((chips,)),
            dma((chips,)),
            dma((6,)),
            dma((chips,)),
            dma((chips,)),
            dma((chips,)),
            dma((heads,)),
            dma((heads,)),
            dma((n,)),
            dma((n,)),
            dma((streams, chips)),
            dma((streams, chips)),
            dma((streams, HALF)),
            dma((streams, HALF)),
            dma((streams, chips)),
            dma((n,)),
            dma((n,)),
        ],
        compiler_params=pltpu.CompilerParams(
            collective_id=0, has_side_effects=True, vmem_limit_bytes=67_043_328
        ),
        name="scores",
    )(group_of, prompt_len, small, q, ck, cv, pk, pv, wt, gain, lm)


def per_device(
    n,
    cont_query,
    cont_key,
    cont_value,
    prefix_key,
    prefix_value,
    out_weight,
    norm_gain,
    lm_head,
    target_ids,
    cont_len,
    prompt_len,
    group_of,
    rewards,
):
    conts, span, _ = cont_query.shape
    own = conts * span
    me = lax.axis_index("seq")
    co = lax.rem(me, CORES)
    lane = jnp.arange(HD, dtype=jnp.int32)
    ids = jnp.tile(target_ids.reshape(own).astype(F32), CORES)
    ids = jnp.where(lane // own == co, ids, 0.0)
    spread_out = jnp.zeros((HD,), F32)
    for a in range(conts):
        spread_out = jnp.where(lane == me * conts + a, rewards[a], spread_out)
    small = jnp.stack([ids, spread_out])
    found = scores_of(
        n,
        group_of,
        prompt_len,
        small,
        cont_query,
        cont_key,
        cont_value,
        prefix_key,
        prefix_value,
        out_weight.T,
        norm_gain.reshape(-1, 1),
        lm_head.T,
    )
    logprob = lax.dynamic_slice_in_dim(found[0], co * own, own).reshape(conts, span)
    position = jnp.arange(span, dtype=jnp.int32)
    token_logprob = jnp.where(position[None, :] < cont_len[:, None], logprob, 0.0)
    every_reward = found[1, : n * conts]
    own_groups = lax.dynamic_slice_in_dim(group_of, me * conts, conts)
    same = (own_groups[:, None] == group_of[None, :]).astype(F32)
    group_mean = jnp.sum(same * every_reward[None, :], axis=1) / GROUP
    deviation = every_reward[None, :] - group_mean[:, None]
    spread = jnp.sqrt(jnp.sum(same * deviation * deviation, axis=1) / (GROUP - 1))
    advantage = (rewards - group_mean) / jnp.maximum(spread, REWARD_FLOOR)
    objective = advantage * jnp.sum(token_logprob, axis=1) / cont_len.astype(F32)
    return (token_logprob, advantage, objective)


def solution(mesh):
    both = ("grp", "seq")
    in_specs = (
        P(both, None, None),
        P(both, None, None),
        P(both, None, None),
        P("grp", "seq", None),
        P("grp", "seq", None),
        P(None, "seq"),
        P(),
        P(None, "seq"),
        P(both, None),
        P(both),
        P("grp"),
        P("grp"),
        P(both),
    )
    out_specs = (P(both, None), P(both), P(both))
    return jax.shard_map(
        functools.partial(per_device, mesh.shape["seq"]),
        mesh=mesh,
        in_specs=in_specs,
        out_specs=out_specs,
        check_vma=False,
    )
```

time: 439 us -> 268 us (0.61)
  Pallas kernels: 0 us -> 254 us
  waiting for transfers between devices: 187 us -> 0 us
  blocking collectives: 98.8 us -> 0 us
  matrix products: 57.4 us -> 0 us
  local copies, waits for them, and re-layouts: 48.8 us -> 6.36 us
  other arithmetic: 30.1 us -> 6.84 us
  between operations: 15.3 us -> 0.66 us
    pallas_call x0 -> x1, Pallas kernels: none -> 254 us  [scores_of(): pl.pallas_call(functools.partial(kernel, dims), out_shape=jax.ShapeDtypeS...]
    all_gather x3 -> x0, waiting for transfers between devices: 187 us -> none  [the longest x1 105 us: sent_together(): whole = lax.all_gather(both, axis, axis=dim, tiled=True)]
    unnamed x2 -> x0, blocking collectives: 66 us -> none
    dot_general x7 -> x0, matrix products: 57.4 us -> none  [the longest x1 35.2 us: shard_stats(): logits = jnp.dot(normed, head, preferred_element_type=jnp.float32)]
    all_gather x2 -> x0, blocking collectives: 32.7 us -> none  [gathered_once(): both, at, found = (lax.all_gather(jnp.concatenate(lines), axis), 0, {})]
    gather x6 -> x0, local copies, waits for them, and re-layouts: 29.1 us -> none  [the longest x3 20.6 us: per_device(): value_piece = jnp.take(pieces[1], own_groups, axis=0)]
    reduce_sum x5 -> x2, other arithmetic: 19 us -> 1.68 us  [the longest x1 0.84 us: per_device(): jnp.sum(same * deviation * deviation, axis=1) / (GROUP - 1)]
    reshape x8 -> x2, local copies, waits for them, and re-layouts: 18.3 us -> 2.25 us  [the longest x1 2.17 us: per_device(): norm_gain.reshape(-1, 1)]
  transfers between devices with their start and end apart: 3 -> 0, of which waited for: 3 -> 0; matrix products, arithmetic and copies ran while one was open for 2% -> 0% of each run, Pallas kernels for 0% -> 0%
where the time goes in v1:
time: 268 us
  Pallas kernels  254 us (95%)
  other arithmetic  6.84 us (3%)
  local copies, waits for them, and re-layouts  6.36 us (2%)
    pallas_call x1, Pallas kernels, scores_of(): pl.pallas_call(functools.partial(kernel, dims), out_shape=jax.ShapeDtypeS...  254 us

profile of v1, /device:TPU:69, one launch (start us, length us, event | category | flops | bytes accessed | tf_op | source)
XLA Modules:
  0.0 267.8 jit_solution(8116783457378756806)
XLA Ops:
  0.6 1.3 dynamic_slice.7
  1.9 0.7 convert_element_type.14
  2.6 0.1 convert_element_type.15
  2.7 0.1 tile.10
  2.8 1.3 fusion.4
  4.1 1.3 compare_select_fusion.3
  5.4 0.6 pad_maximum_fusion.small
  5.9 2.2 reshape.103.gain
  8.1 254.0 %scores.1 = f32[2,128]{1,0:T(2,128)} custom-call(s32[64]{0:T(128)} %group_of.1, s32[4]{0:T(128)} %prompt_len.1, f32[2,128]{1,0:T(2,128)} %pad_maximum_fusion.small, bf16[2,32,2560]{2,1,0:T(8,128)(2,1)} %q.1, bf16[2,32,512]{2,1,0:T(8,128)(2,1)} %ck.1, bf16[2,32,512]{2,1,0:T(8,128)(2,1)} %cv.1, bf16[4,64,512]{2,1,0:T(8,128)(2,1)} %pk.1, ...), custom_call_target="tpu_custom_call" | custom-call | tf_op jit(solution)/shard_map/scores/pallas_call | solution.py:700
  262.1 0.6 slice_bitcast_fusion
  262.7 0.6 slice.14
  263.4 0.1 dynamic-slice_reduce_fusion
  263.5 0.8 fusion.2
  264.3 0.8 fusion.1
  265.1 0.1 reshape.102
  265.2 1.4 fusion.3
  266.6 1.2 convert_divide_fusion
  (2 shorter events, 0.0 us)

commit v2 on v1

--- a/solution.py
+++ b/solution.py
@@ -15,8 +15,10 @@
 
 CORES = 2
 CHUNKS = 4
-SKEW = 3
+SKEW = 2
+PER_SLOT = 3
 TILE = 480
+WEIGH = 160
 HALF = 8
 
 BF16 = jnp.bfloat16
@@ -42,28 +44,32 @@
     dims,
     group_of,
     prompt_len,
-    small,
+    rewards,
+    cont_len,
+    groups,
+    ids,
+    gain,
     q,
     ck,
     cv,
     pk,
     pv,
     wt,
-    gain,
     lm,
-    out,
+    out_logprob,
+    out_advantage,
+    out_objective,
     kvs,
     kvr,
     qs,
     qr,
     ab,
     hb,
-    nt,
     wv,
-    gv,
     lv,
     smv,
     smg,
+    run_f,
     run_m,
     run_s,
     run_p,
@@ -142,7 +148,18 @@
         return carry
 
     lax.fori_loop(0, heads, load_q, 0)
-    pltpu.make_async_copy(small, smv, loc.at[2]).start()
+
+    lane = lax.broadcasted_iota(jnp.int32, (1, HD), 1)
+    own_ids = ids[...].astype(F32)
+    own_ids = jnp.concatenate([own_ids[a : a + 1, :] for a in range(conts)] * CORES, axis=1)
+    own_ids = jnp.where(lax.div(lane, own) == co, own_ids, 0.0)
+    own_rewards = jnp.zeros((1, HD), F32)
+    for a in range(conts):
+        own_rewards = jnp.where(lane == me * conts + a, rewards[a], own_rewards)
+    smv[0:1, :] = own_ids
+    smv[1:2, :] = own_rewards
+    smg[me, 0:1, :] = own_ids
+    smg[me, 1:2, :] = own_rewards
 
     barrier = pltpu.get_barrier_semaphore()
 
@@ -155,9 +172,10 @@
 
         return carry
 
-    lax.fori_loop(0, n, greet, 0)
-    pltpu.make_async_copy(kvs, kvs, loc.at[0]).wait()
-    pl.semaphore_wait(barrier, n - 1)
+    with jax.named_scope("greet"):
+        lax.fori_loop(0, n, greet, 0)
+        pltpu.make_async_copy(kvs, kvs, loc.at[0]).wait()
+        pl.semaphore_wait(barrier, n - 1)
 
     def kv_at(src):
         rows = pl.ds(pl.multiple_of((chip(src) * CORES + co) * positions, positions), positions)
@@ -216,6 +234,9 @@
 
     def q_send(step):
         target = chip(z + side * step)
+        if 2 * step == heads:
+            shifted = jnp.where(j >= side // 2, side * step - side // 2, side * step + side // 2)
+            target = chip(z + shifted)
         return send(
             qs.at[lax.div(target, side)],
             qr.at[k0],
@@ -237,7 +258,6 @@
     for source, rows in keep_q:
         pltpu.make_async_copy(source, qr.at[k0, rows, :], loc.at[5]).start()
 
-    pltpu.make_async_copy(small, smv, loc.at[2]).wait()
 
     def small_send(d):
         return send(smv, smg.at[me], sm_ss.at[d], sm_rs.at[me], d)
@@ -249,14 +269,11 @@
 
         return carry
 
-    lax.fori_loop(0, n, small_out, 0)
-    keep_small = pltpu.make_async_copy(small, smg.at[me], loc.at[2])
-    keep_small.start()
+    with jax.named_scope("small"):
+        lax.fori_loop(0, n, small_out, 0)
     load_w = pltpu.make_async_copy(wt, wv, loc.at[6])
     load_w.start()
-    load_gain = pltpu.make_async_copy(gain, gv, loc.at[7])
-    load_gain.start()
-    load_lm = pltpu.make_async_copy(lm, lv.at[pl.ds(0, vocab), :], loc.at[8])
+    load_lm = pltpu.make_async_copy(lm, lv.at[pl.ds(0, vocab), :], loc.at[2])
     load_lm.start()
 
     reach = side + side // 2
@@ -293,7 +310,8 @@
         return carry
 
     longest = side - 1 + reach
-    lax.fori_loop(0, longest, chain, 0)
+    with jax.named_scope("chain"):
+        lax.fori_loop(0, longest, chain, 0)
 
     keep_k.wait()
     keep_v.wait()
@@ -309,7 +327,8 @@
         send(other_rows(src), other_rows(src), kv_sd.at[src], kv_rd.at[src], partner).wait_recv()
         return carry
 
-    lax.fori_loop(0, chips, kv_partner, 0)
+    with jax.named_scope("kvpartner"):
+        lax.fori_loop(0, chips, kv_partner, 0)
 
     def q_arrived(c, carry):
         @pl.when(c != k0)
@@ -318,12 +337,24 @@
 
         return carry
 
-    lax.fori_loop(0, heads, q_arrived, 0)
+    with jax.named_scope("qarrive"):
+        lax.fori_loop(0, heads, q_arrived, 0)
+
+    def place_of(c, chip_id):
+        k = lax.div(chip_id, side)
+        away = lax.rem(c - k + heads, heads)
+        place = lax.rem(chip_id, side)
+        return jnp.where(2 * away == heads, lax.rem(place + side // 2, side), place)
+
+    def token_row(c, chip_id, core):
+        k = lax.div(chip_id, side)
+        return ((k * side + place_of(c, chip_id)) * CORES + core) * own
 
     def block_at(stream, chip_id, core):
         d = chip(chip_id) * CORES + core
         if stream < CHUNKS:
-            return ab.at[stream, pl.ds(pl.multiple_of(d * own, own), own), :]
+            at = token_row(stream, chip(chip_id), core)
+            return ab.at[stream, pl.ds(pl.multiple_of(at, own), own), :]
         return hb.at[stream - CHUNKS, pl.ds(pl.multiple_of(d * feats, 16), feats), :]
 
     def ring_send(stream, source, target, send_sem):
@@ -390,7 +421,7 @@
 
     def attention(c):
         for a in range(conts):
-            cont = ((c * side + j) * CORES + co) * conts + a
+            cont = ((c * side + place_of(c, z)) * CORES + co) * conts + a
             g = group_of[cont]
             length = prompt_len[g]
             queries = qr[c, pl.ds(a * one_q, one_q), :]
@@ -411,7 +442,7 @@
             mixed = jnp.dot(weights.astype(BF16), kvr[1, g], preferred_element_type=F32)
             mixed += jnp.dot(near.astype(BF16), own_values, preferred_element_type=F32)
             mixed = (mixed / total).astype(BF16)
-            rows = pl.ds(pl.multiple_of(me * own + a * span, span), span)
+            rows = pl.ds(pl.multiple_of(token_row(c, z, co) + a * span, span), span)
             for g5 in range(per_head):
                 ab[c, rows, g5 * HD : (g5 + 1) * HD] = mixed[g5 * span : (g5 + 1) * span, :]
 
@@ -432,14 +463,11 @@
             return total + jnp.sum(x * x, axis=0, keepdims=True)
 
         total = lax.fori_loop(0, features // strip, squares, jnp.zeros((1, chunk_rows), F32))
-        factor = lax.rsqrt(total / features + EPSILON)
-
-        def scale(i, carry):
-            rows = pl.ds(pl.multiple_of(i * strip, strip), strip)
-            nt[rows, :] = (hb[c, rows, :].astype(F32) * factor * gv[rows, :]).astype(BF16)
-            return carry
-
-        lax.fori_loop(0, features // strip, scale, 0)
+        run_f[...] = lax.rsqrt(total / features + EPSILON)
+
+    def weigh(i):
+        rows = pl.ds(pl.multiple_of(i * WEIGH, 16), WEIGH)
+        lv[rows, :] = (lv[rows, :].astype(F32) * gain[...]).astype(BF16)
 
     def chunk_ids(c):
         rows = []
@@ -451,7 +479,7 @@
 
     def tile(c, v):
         rows = pl.ds(pl.multiple_of(v * TILE, 16), TILE)
-        logits = jnp.dot(lv[rows, :], nt[...], preferred_element_type=F32)
+        logits = jnp.dot(lv[rows, :], hb[c], preferred_element_type=F32) * run_f[...]
         at = lax.broadcasted_iota(jnp.int32, logits.shape, 0) + v * TILE
         logits = jnp.where(at < vocab, logits, NEGATIVE)
         run_p[...] += jnp.sum(jnp.where(at == chunk_ids(c), logits, 0.0), axis=0, keepdims=True)
@@ -493,7 +521,15 @@
                     copy.start()
 
     tiles = -(-vocab // TILE)
-    per_slot = -(-(tiles - 1) // (SKEW - 1))
+    steps = []
+    finished = 0
+    while finished < tiles * CHUNKS:
+        at = len(steps)
+        steps.append(finished)
+        ready = sum(at >= 2 * HALF + SKEW * c for c in range(CHUNKS)) * tiles
+        finished = min(finished + PER_SLOT, ready)
+    slots = len(steps)
+    steps.append(finished)
 
     def slot(i, carry):
         for stream in range(CHUNKS, 2 * CHUNKS):
@@ -501,18 +537,21 @@
 
             @pl.when(jnp.logical_and(t >= 1, t <= HALF))
             def _(stream=stream, t=t):
-                ring_step(stream, t)
+                with jax.named_scope(f"hid{stream}"):
+                    ring_step(stream, t)
 
         for stream in range(CHUNKS):
             t = i - SKEW * stream
 
             @pl.when(jnp.logical_and(t >= 1, t <= HALF))
             def _(stream=stream, t=t):
-                ring_step(stream, t)
+                with jax.named_scope(f"att{stream}"):
+                    ring_step(stream, t)
 
         @pl.when(jnp.logical_and(lax.rem(i, SKEW) == 0, i < SKEW * CHUNKS))
         def _():
-            attention(lax.div(i, SKEW))
+            with jax.named_scope("attention"):
+                attention(lax.div(i, SKEW))
 
         for c in range(CHUNKS):
 
@@ -524,22 +563,29 @@
         def _():
             load_w.wait()
 
+        @pl.when(i == 0)
+        def _():
+            load_lm.wait()
+
+        @pl.when(i < lv.shape[0] // WEIGH)
+        def _():
+            with jax.named_scope("weigh"):
+                weigh(i)
+
         for c in range(CHUNKS):
 
             @pl.when(i == SKEW * c + HALF)
             def _(c=c):
-                ring_partner(c)
-                project(c)
+                with jax.named_scope("partner1"):
+                    ring_partner(c)
+                with jax.named_scope("project"):
+                    project(c)
                 ring_open(CHUNKS + c)
 
         m = i - 2 * HALF
 
         @pl.when(m == 0)
         def _():
-            load_gain.wait()
-            load_lm.wait()
-            keep_small.wait()
-
             def small_in(d, carry):
                 @pl.when(d != me)
                 def _():
@@ -553,39 +599,52 @@
 
             @pl.when(m == SKEW * c)
             def _(c=c):
-                ring_partner(CHUNKS + c)
-
-        @pl.when(m >= 0)
-        def _():
-            c = lax.div(m, SKEW)
-            r = lax.rem(m, SKEW)
-
-            @pl.when(r == 0)
+                with jax.named_scope("partner2"):
+                    ring_partner(CHUNKS + c)
+
+        first = 0
+        last = 0
+        for at in range(2 * HALF, slots):
+            first = first + jnp.where(i > at, steps[at + 1] - steps[at], 0)
+            last = last + jnp.where(i >= at, steps[at + 1] - steps[at], 0)
+
+        def one(step, carry):
+            c = lax.div(step, tiles)
+            v = lax.rem(step, tiles)
+
+            @pl.when(v == 0)
             def _():
-                normalize(c)
+                with jax.named_scope("norm"):
+                    normalize(c)
                 run_m[...] = jnp.full_like(run_m, NEGATIVE)
                 run_s[...] = jnp.zeros_like(run_s)
                 run_p[...] = jnp.zeros_like(run_p)
 
-            first = jnp.maximum(1 + (r - 1) * per_slot, 0)
-            first = jnp.where(r == 0, 0, first)
-            last = jnp.minimum(1 + r * per_slot, tiles)
-
-            def one(v, carry):
+            with jax.named_scope("tile"):
                 tile(c, v)
-                return carry
-
-            lax.fori_loop(first, last, one, 0)
-
-        for c in range(CHUNKS):
-
-            @pl.when(m == SKEW * c + SKEW - 1)
-            def _(c=c):
-                stats_out(c)
-
-        return carry
-
-    lax.fori_loop(0, 2 * HALF + SKEW * CHUNKS, slot, 0)
+
+            @pl.when(v == tiles - 1)
+            def _():
+                with jax.named_scope("stats"):
+                    stats_out(c)
+
+            return carry
+
+        lax.fori_loop(first, last, one, 0)
+        return carry
+
+    with jax.named_scope("slots"):
+        lax.fori_loop(0, slots, slot, 0)
+
+    every_reward = jnp.sum(smg[...][:, 1, :], axis=0, keepdims=True)[:, 0 : n * conts]
+    advantages = []
+    for a in range(conts):
+        same = groups[...] == group_of[me * conts + a]
+        mean = jnp.sum(jnp.where(same, every_reward, 0.0), axis=1, keepdims=True) / GROUP
+        off = every_reward - mean
+        spread = jnp.sum(jnp.where(same, off * off, 0.0), axis=1, keepdims=True)
+        spread = jnp.sqrt(spread / (GROUP - 1))
+        advantages.append((rewards[a] - mean) / jnp.maximum(spread, REWARD_FLOOR))
 
     def stats_in(d, carry):
         @pl.when(d != me)
@@ -594,13 +653,22 @@
 
         return carry
 
-    lax.fori_loop(0, n, stats_in, 0)
+    with jax.named_scope("join"):
+        lax.fori_loop(0, n, stats_in, 0)
     everyone = sr[...]
     lse = everyone[:, 0, :]
     peak = jnp.max(lse, axis=0, keepdims=True)
     lse = peak + jnp.log(jnp.sum(jnp.exp(lse - peak), axis=0, keepdims=True))
-    out[0:1, :] = jnp.sum(everyone[:, 1, :], axis=0, keepdims=True) - lse
-    out[1:2, :] = jnp.sum(smg[...][:, 1, :], axis=0, keepdims=True)
+    logprob = jnp.sum(everyone[:, 1, :], axis=0, keepdims=True) - lse
+    logprob = jnp.where(co == 0, logprob[:, 0:own], logprob[:, own : 2 * own])
+    position = lax.broadcasted_iota(jnp.int32, (1, span), 1)
+    for a in range(conts):
+        live = jnp.where(position < cont_len[a], logprob[:, a * span : (a + 1) * span], 0.0)
+        out_logprob[a : a + 1, :] = live
+        gained = advantages[a] * jnp.sum(live, axis=1, keepdims=True)
+        gained = gained / jnp.full((1, 1), cont_len[a], jnp.int32).astype(F32)
+        out_advantage[a] = advantages[a][0, 0]
+        out_objective[a] = gained[0, 0]
 
     @pl.when(j >= side // 2)
     def _():
@@ -678,7 +746,7 @@
 
 
 def scores_of(
-    n, group_of, prompt_len, small, q, ck, cv, pk, pv, wt, gain, lm
+    n, group_of, prompt_len, rewards, cont_len, groups, ids, gain, q, ck, cv, pk, pv, wt, lm
 ):
     conts, span, query_width = q.shape
     prompts, positions, kv_width = pk.shape
@@ -697,11 +765,16 @@
     vmem_rows = -(-vocab // TILE) * TILE
     any_spec = pl.BlockSpec(memory_space=pl.ANY)
     smem_spec = pl.BlockSpec(memory_space=pltpu.SMEM)
+    vmem_spec = pl.BlockSpec(memory_space=pltpu.VMEM)
     return pl.pallas_call(
         functools.partial(kernel, dims),
-        out_shape=jax.ShapeDtypeStruct((2, HD), F32),
-        in_specs=[smem_spec] * 2 + [any_spec] * 9,
-        out_specs=pl.BlockSpec(memory_space=pltpu.VMEM),
+        out_shape=(
+            jax.ShapeDtypeStruct((conts, span), F32),
+            jax.ShapeDtypeStruct((conts,), F32),
+            jax.ShapeDtypeStruct((conts,), F32),
+        ),
+        in_specs=[smem_spec] * 4 + [vmem_spec] * 3 + [any_spec] * 7,
+        out_specs=(vmem_spec, smem_spec, smem_spec),
         scratch_shapes=[
             pltpu.VMEM((heads, 2, prompts, positions, HD), BF16),
             pltpu.VMEM((2, prompts, n * positions, HD), BF16),
@@ -709,12 +782,11 @@
             pltpu.VMEM((heads, chunk_q, HD), BF16),
             pltpu.VMEM((CHUNKS, n * own, per_head * HD), BF16),
             pltpu.VMEM((CHUNKS, n * feats, chunk_rows), BF16),
-            pltpu.VMEM((n * feats, chunk_rows), BF16),
             pltpu.VMEM((feats, features), BF16),
-            pltpu.VMEM((n * feats, 1), F32),
             pltpu.VMEM((vmem_rows, n * feats), BF16),
             pltpu.VMEM((2, HD), F32),
             pltpu.VMEM((n, 2, HD), F32),
+            pltpu.VMEM((1, chunk_rows), F32),
             pltpu.VMEM((1, chunk_rows), F32),
             pltpu.VMEM((1, chunk_rows), F32),
             pltpu.VMEM((1, chunk_rows), F32),
@@ -743,7 +815,7 @@
             collective_id=0, has_side_effects=True, vmem_limit_bytes=67_043_328
         ),
         name="scores",
-    )(group_of, prompt_len, small, q, ck, cv, pk, pv, wt, gain, lm)
+    )(group_of, prompt_len, rewards, cont_len, groups, ids, gain, q, ck, cv, pk, pv, wt, lm)
 
 
 def per_device(
@@ -762,43 +834,23 @@
     group_of,
     rewards,
 ):
-    conts, span, _ = cont_query.shape
-    own = conts * span
-    me = lax.axis_index("seq")
-    co = lax.rem(me, CORES)
-    lane = jnp.arange(HD, dtype=jnp.int32)
-    ids = jnp.tile(target_ids.reshape(own).astype(F32), CORES)
-    ids = jnp.where(lane // own == co, ids, 0.0)
-    spread_out = jnp.zeros((HD,), F32)
-    for a in range(conts):
-        spread_out = jnp.where(lane == me * conts + a, rewards[a], spread_out)
-    small = jnp.stack([ids, spread_out])
-    found = scores_of(
+    return scores_of(
         n,
         group_of,
         prompt_len,
-        small,
+        rewards,
+        cont_len,
+        group_of.reshape(1, -1),
+        target_ids,
+        norm_gain.reshape(1, -1),
         cont_query,
         cont_key,
         cont_value,
         prefix_key,
         prefix_value,
         out_weight.T,
-        norm_gain.reshape(-1, 1),
         lm_head.T,
     )
-    logprob = lax.dynamic_slice_in_dim(found[0], co * own, own).reshape(conts, span)
-    position = jnp.arange(span, dtype=jnp.int32)
-    token_logprob = jnp.where(position[None, :] < cont_len[:, None], logprob, 0.0)
-    every_reward = found[1, : n * conts]
-    own_groups = lax.dynamic_slice_in_dim(group_of, me * conts, conts)
-    same = (own_groups[:, None] == group_of[None, :]).astype(F32)
-    group_mean = jnp.sum(same * every_reward[None, :], axis=1) / GROUP
-    deviation = every_reward[None, :] - group_mean[:, None]
-    spread = jnp.sqrt(jnp.sum(same * deviation * deviation, axis=1) / (GROUP - 1))
-    advantage = (rewards - group_mean) / jnp.maximum(spread, REWARD_FLOOR)
-    objective = advantage * jnp.sum(token_logprob, axis=1) / cont_len.astype(F32)
-    return (token_logprob, advantage, objective)
 
 
 def solution(mesh):

time: 268 us -> 257 us (0.959)
  other arithmetic: 6.84 us -> 0 us
  Pallas kernels: 254 us -> 251 us
    unnamed x0 -> x3, local copies, waits for them, and re-layouts: none -> 3.54 us
    reduce_sum x3 -> x0, other arithmetic: 3.08 us -> none  [the longest x1 1.4 us: per_device(): jnp.sum(token_logprob, axis=1)]
where the time goes in v2:
time: 257 us
  Pallas kernels  251 us (98%)
  local copies, waits for them, and re-layouts  4.84 us (2%)
    pallas_call x1, Pallas kernels, scores_of(): pl.pallas_call(functools.partial(kernel, dims), out_shape=(jax.ShapeDtype...  251 us

profile of v2, /device:TPU:69, one launch (start us, length us, event | category | flops | bytes accessed | tf_op | source)
XLA Modules:
  0.0 257.0 jit_solution(10124447300475705983)
XLA Ops:
  0.6 1.3 reshape.13.gain
  1.9 251.5 %scores.1 = (f32[2,32]{1,0:T(2,128)}, f32[2]{0:T(128)}, f32[2]{0:T(128)}) custom-call(s32[64]{0:T(128)} %group_of.1, s32[4]{0:T(128)} %prompt_len.1, f32[2]{0:T(128)} %rewards.1, s32[2]{0:T(128)} %cont_len.1, s32[1,64]{1,0:T(1,128)} %bitcast.5, s32[2,32]{1,0:T(2,128)} %ids.1, f32[1,2560]{1,0:T(1,128)} %reshape.13.gain, bf16[2,32,2560]{2,1,0:T(8,128)(2,1)} %q.1, ...), custom_call_target="tpu_custom_call" | custom-call | tf_op jit(solution)/shard_map/scores/pallas_call | solution.py:769
  253.4 1.2 copy.19
  254.6 1.2 copy.20
  255.8 1.1 copy.21

commit v3 on v2

--- a/solution.py
+++ b/solution.py
@@ -13,10 +13,11 @@
 EPSILON = 1e-06
 REWARD_FLOOR = 0.25
 
+Q_AT = (0, 3, 5, 3)
 CORES = 2
 CHUNKS = 4
-SKEW = 2
-PER_SLOT = 3
+STARTS = (0, 0, 5, 7)
+PER_SLOT = 2
 TILE = 480
 WEIGH = 160
 HALF = 8
@@ -203,17 +204,6 @@
     far_left = kv_send(z, kvs.at[far_head], base - side - 1, kv_so.at[5])
     own_part = kv_d2d(z, kvs.at[k0])
 
-    @pl.when(j >= side // 2)
-    def _():
-        far_right.start()
-
-    @pl.when(j < side // 2)
-    def _():
-        far_left.start()
-
-    ext_right.start()
-    ext_left.start()
-
     @pl.when(j < side - 1)
     def _():
         own_right.start()
@@ -245,9 +235,6 @@
             dev(target),
         )
 
-    for step in range(1, heads):
-        q_send(step).start()
-
     keep_q = []
     for a in range(conts):
         for g in range(per_head):
@@ -284,8 +271,32 @@
     def down_send(t):
         return kv_send(z + t, kv_at(z + t), z - 1, kv_sn.at[t - 1])
 
+    def depart(i):
+        @pl.when(i == side - 1 - j)
+        def _():
+            ext_right.start()
+
+        @pl.when(i == j)
+        def _():
+            ext_left.start()
+
+        @pl.when(jnp.logical_and(j >= side // 2, i == 2 * (side - 1) - j))
+        def _():
+            far_right.start()
+
+        @pl.when(jnp.logical_and(j < side // 2, i == side - 1 + j))
+        def _():
+            far_left.start()
+
+        for step in range(1, heads):
+
+            @pl.when(i == Q_AT[step])
+            def _(step=step):
+                q_send(step).start()
+
     def chain(i, carry):
         t = i + 1
+        depart(i)
 
         @pl.when(t <= j + reach)
         def _():
@@ -381,6 +392,13 @@
         ring_right(stream, 0).start()
         ring_left(stream, 0).start()
         ring_d2d(stream, z).start()
+
+    def attended_open(c):
+        rows = pl.ds(pl.multiple_of(token_row(c, z, co), own), own)
+        block = ab.at[c, rows, :]
+        send(block, block, g_sr.at[c, 0], g_rs.at[c, z], dev(z + 1)).start()
+        send(block, block, g_sl.at[c, 0], g_rs.at[c, z], dev(z - 1)).start()
+        send(block, block, g_sd.at[c, z], g_rd.at[c, z], partner).start()
 
     def ring_step(stream, t):
         right, left = steps_of(stream)
@@ -526,14 +544,14 @@
     while finished < tiles * CHUNKS:
         at = len(steps)
         steps.append(finished)
-        ready = sum(at >= 2 * HALF + SKEW * c for c in range(CHUNKS)) * tiles
+        ready = sum(at >= 2 * HALF + start for start in STARTS) * tiles
         finished = min(finished + PER_SLOT, ready)
     slots = len(steps)
     steps.append(finished)
 
     def slot(i, carry):
         for stream in range(CHUNKS, 2 * CHUNKS):
-            t = i - (SKEW * (stream - CHUNKS) + HALF)
+            t = i - (STARTS[stream - CHUNKS] + HALF)
 
             @pl.when(jnp.logical_and(t >= 1, t <= HALF))
             def _(stream=stream, t=t):
@@ -541,23 +559,22 @@
                     ring_step(stream, t)
 
         for stream in range(CHUNKS):
-            t = i - SKEW * stream
+            t = i - STARTS[stream]
 
             @pl.when(jnp.logical_and(t >= 1, t <= HALF))
             def _(stream=stream, t=t):
                 with jax.named_scope(f"att{stream}"):
                     ring_step(stream, t)
 
-        @pl.when(jnp.logical_and(lax.rem(i, SKEW) == 0, i < SKEW * CHUNKS))
-        def _():
+        def begin(c, carry):
             with jax.named_scope("attention"):
-                attention(lax.div(i, SKEW))
-
-        for c in range(CHUNKS):
-
-            @pl.when(i == SKEW * c)
-            def _(c=c):
-                ring_open(c)
+                attention(c)
+            attended_open(c)
+            return carry
+
+        begun = sum((i > start).astype(jnp.int32) for start in STARTS)
+        due = sum((i >= start).astype(jnp.int32) for start in STARTS)
+        lax.fori_loop(begun, due, begin, 0)
 
         @pl.when(i == HALF)
         def _():
@@ -574,7 +591,7 @@
 
         for c in range(CHUNKS):
 
-            @pl.when(i == SKEW * c + HALF)
+            @pl.when(i == STARTS[c] + HALF)
             def _(c=c):
                 with jax.named_scope("partner1"):
                     ring_partner(c)
@@ -597,7 +614,7 @@
 
         for c in range(CHUNKS):
 
-            @pl.when(m == SKEW * c)
+            @pl.when(m == STARTS[c])
             def _(c=c):
                 with jax.named_scope("partner2"):
                     ring_partner(CHUNKS + c)

time: 257 us -> 242 us (0.942)
  Pallas kernels: 251 us -> 236 us
    pallas_call x1, Pallas kernels: 251 us -> 236 us  [scores_of(): pl.pallas_call(functools.partial(kernel, dims), out_shape=(jax.ShapeDtype...]
where the time goes in v3:
time: 242 us
  Pallas kernels  236 us (98%)
  local copies, waits for them, and re-layouts  4.84 us (2%)
    pallas_call x1, Pallas kernels, scores_of(): pl.pallas_call(functools.partial(kernel, dims), out_shape=(jax.ShapeDtype...  236 us

profile of v3, /device:TPU:69, one launch (start us, length us, event | category | flops | bytes accessed | tf_op | source)
XLA Modules:
  0.0 242.0 jit_solution(10859597799559036020)
XLA Ops:
  0.6 1.3 reshape.13.gain
  1.9 236.5 %scores.1 = (f32[2,32]{1,0:T(2,128)}, f32[2]{0:T(128)}, f32[2]{0:T(128)}) custom-call(s32[64]{0:T(128)} %group_of.1, s32[4]{0:T(128)} %prompt_len.1, f32[2]{0:T(128)} %rewards.1, s32[2]{0:T(128)} %cont_len.1, s32[1,64]{1,0:T(1,128)} %bitcast.5, s32[2,32]{1,0:T(2,128)} %ids.1, f32[1,2560]{1,0:T(1,128)} %reshape.13.gain, bf16[2,32,2560]{2,1,0:T(8,128)(2,1)} %q.1, ...), custom_call_target="tpu_custom_call" | custom-call | tf_op jit(solution)/shard_map/scores/pallas_call | solution.py:786
  238.4 1.2 copy.19
  239.7 1.2 copy.20
  240.8 1.1 copy.21

commit v4 on v3

--- a/solution.py
+++ b/solution.py
@@ -19,6 +19,7 @@
 STARTS = (0, 0, 5, 7)
 PER_SLOT = 2
 TILE = 480
+PIECES = 3
 WEIGH = 160
 HALF = 8
 
@@ -496,17 +497,24 @@
         return jnp.where(ids < vocab, ids, -1)
 
     def tile(c, v):
-        rows = pl.ds(pl.multiple_of(v * TILE, 16), TILE)
-        logits = jnp.dot(lv[rows, :], hb[c], preferred_element_type=F32) * run_f[...]
-        at = lax.broadcasted_iota(jnp.int32, logits.shape, 0) + v * TILE
-        logits = jnp.where(at < vocab, logits, NEGATIVE)
-        run_p[...] += jnp.sum(jnp.where(at == chunk_ids(c), logits, 0.0), axis=0, keepdims=True)
-        old = run_m[...]
-        new = jnp.maximum(old, jnp.max(logits, axis=0, keepdims=True))
-        run_s[...] = run_s[...] * jnp.exp(old - new) + jnp.sum(
-            jnp.exp(logits - new), axis=0, keepdims=True
-        )
-        run_m[...] = new
+        ids_row = chunk_ids(c)
+        part = TILE // PIECES
+        peak, mass, hit = run_m[...], run_s[...], run_p[...]
+        for piece in range(PIECES):
+            first_row = v * TILE + piece * part
+            rows = pl.ds(pl.multiple_of(first_row, 16), part)
+            logits = jnp.dot(lv[rows, :], hb[c], preferred_element_type=F32) * run_f[...]
+            at = lax.broadcasted_iota(jnp.int32, logits.shape, 0) + first_row
+            logits = jnp.where(at < vocab, logits, NEGATIVE)
+            hit += jnp.sum(jnp.where(at == ids_row, logits, 0.0), axis=0, keepdims=True)
+            new = jnp.maximum(peak, jnp.max(logits, axis=0, keepdims=True))
+            mass = mass * jnp.exp(peak - new) + jnp.sum(
+                jnp.exp(logits - new), axis=0, keepdims=True
+            )
+            peak = new
+        run_m[...] = peak
+        run_s[...] = mass
+        run_p[...] = hit
 
     def stats_send(c, i, core):
         d = (c * side + i) * CORES + core
@@ -550,20 +558,20 @@
     steps.append(finished)
 
     def slot(i, carry):
+        for stream in range(CHUNKS):
+            t = i - STARTS[stream]
+
+            @pl.when(jnp.logical_and(t >= 1, t <= HALF))
+            def _(stream=stream, t=t):
+                with jax.named_scope(f"att{stream}"):
+                    ring_step(stream, t)
+
         for stream in range(CHUNKS, 2 * CHUNKS):
             t = i - (STARTS[stream - CHUNKS] + HALF)
 
             @pl.when(jnp.logical_and(t >= 1, t <= HALF))
             def _(stream=stream, t=t):
                 with jax.named_scope(f"hid{stream}"):
-                    ring_step(stream, t)
-
-        for stream in range(CHUNKS):
-            t = i - STARTS[stream]
-
-            @pl.when(jnp.logical_and(t >= 1, t <= HALF))
-            def _(stream=stream, t=t):
-                with jax.named_scope(f"att{stream}"):
                     ring_step(stream, t)
 
         def begin(c, carry):

time: 242 us -> 240 us (level)
    pallas_call x1, Pallas kernels: 236 us -> 234 us  [scores_of(): pl.pallas_call(functools.partial(kernel, dims), out_shape=(jax.ShapeDtype...]
where the time goes in v4:
time: 240 us; the launch traced here: 239 us
  Pallas kernels  234 us (98%)
  local copies, waits for them, and re-layouts  4.84 us (2%)
    pallas_call x1, Pallas kernels, scores_of(): pl.pallas_call(functools.partial(kernel, dims), out_shape=(jax.ShapeDtype...  234 us

profile of v4, /device:TPU:69, one launch (start us, length us, event | category | flops | bytes accessed | tf_op | source)
XLA Modules:
  0.0 239.4 jit_solution(14738140946759695191)
XLA Ops:
  0.6 1.3 reshape.13.gain
  1.9 233.9 %scores.1 = (f32[2,32]{1,0:T(2,128)}, f32[2]{0:T(128)}, f32[2]{0:T(128)}) custom-call(s32[64]{0:T(128)} %group_of.1, s32[4]{0:T(128)} %prompt_len.1, f32[2]{0:T(128)} %rewards.1, s32[2]{0:T(128)} %cont_len.1, s32[1,64]{1,0:T(1,128)} %bitcast.5, s32[2,32]{1,0:T(2,128)} %ids.1, f32[1,2560]{1,0:T(1,128)} %reshape.13.gain, bf16[2,32,2560]{2,1,0:T(8,128)(2,1)} %q.1, ...), custom_call_target="tpu_custom_call" | custom-call | tf_op jit(solution)/shard_map/scores/pallas_call | solution.py:794
  235.8 1.2 copy.19
  237.0 1.2 copy.20
  238.2 1.1 copy.21

commit v5 on v4

--- a/solution.py
+++ b/solution.py
@@ -58,9 +58,7 @@
     pv,
     wt,
     lm,
-    out_logprob,
-    out_advantage,
-    out_objective,
+    out,
     kvs,
     kvr,
     qs,
@@ -68,6 +66,7 @@
     ab,
     hb,
     wv,
+    gv,
     lv,
     smv,
     smg,
@@ -121,6 +120,19 @@
     def dev(at):
         return chip(at) * CORES + co
 
+    barrier = pltpu.get_barrier_semaphore()
+
+    def greet(d, carry):
+        @pl.when(d != me)
+        def _():
+            pl.semaphore_signal(
+                barrier, inc=1, device_id={"seq": d}, device_id_type=pl.DeviceIdType.MESH
+            )
+
+        return carry
+
+    lax.fori_loop(0, n, greet, 0)
+
     def kv_loads(head):
         lanes = pl.ds(pl.multiple_of(head * HD, HD), HD)
         return lanes
@@ -163,19 +175,7 @@
     smg[me, 0:1, :] = own_ids
     smg[me, 1:2, :] = own_rewards
 
-    barrier = pltpu.get_barrier_semaphore()
-
-    def greet(d, carry):
-        @pl.when(d != me)
-        def _():
-            pl.semaphore_signal(
-                barrier, inc=1, device_id={"seq": d}, device_id_type=pl.DeviceIdType.MESH
-            )
-
-        return carry
-
     with jax.named_scope("greet"):
-        lax.fori_loop(0, n, greet, 0)
         pltpu.make_async_copy(kvs, kvs, loc.at[0]).wait()
         pl.semaphore_wait(barrier, n - 1)
 
@@ -486,7 +486,7 @@
 
     def weigh(i):
         rows = pl.ds(pl.multiple_of(i * WEIGH, 16), WEIGH)
-        lv[rows, :] = (lv[rows, :].astype(F32) * gain[...]).astype(BF16)
+        lv[rows, :] = (lv[rows, :].astype(F32) * gv[...]).astype(BF16)
 
     def chunk_ids(c):
         rows = []
@@ -591,6 +591,8 @@
         @pl.when(i == 0)
         def _():
             load_lm.wait()
+            for row in range(gain.shape[0]):
+                gv[0:1, row * HD : (row + 1) * HD] = gain[row : row + 1, :]
 
         @pl.when(i < lv.shape[0] // WEIGH)
         def _():
@@ -687,13 +689,17 @@
     logprob = jnp.sum(everyone[:, 1, :], axis=0, keepdims=True) - lse
     logprob = jnp.where(co == 0, logprob[:, 0:own], logprob[:, own : 2 * own])
     position = lax.broadcasted_iota(jnp.int32, (1, span), 1)
+    gains = jnp.zeros((1, HD), F32)
+    objectives = jnp.zeros((1, HD), F32)
     for a in range(conts):
         live = jnp.where(position < cont_len[a], logprob[:, a * span : (a + 1) * span], 0.0)
-        out_logprob[a : a + 1, :] = live
+        out[a : a + 1, 0:span] = live
         gained = advantages[a] * jnp.sum(live, axis=1, keepdims=True)
         gained = gained / jnp.full((1, 1), cont_len[a], jnp.int32).astype(F32)
-        out_advantage[a] = advantages[a][0, 0]
-        out_objective[a] = gained[0, 0]
+        gains = jnp.where(lane == a, advantages[a], gains)
+        objectives = jnp.where(lane == a, gained, objectives)
+    out[conts : conts + 1, :] = gains
+    out[conts + 1 : conts + 2, :] = objectives
 
     @pl.when(j >= side // 2)
     def _():
@@ -793,13 +799,9 @@
     vmem_spec = pl.BlockSpec(memory_space=pltpu.VMEM)
     return pl.pallas_call(
         functools.partial(kernel, dims),
-        out_shape=(
-            jax.ShapeDtypeStruct((conts, span), F32),
-            jax.ShapeDtypeStruct((conts,), F32),
-            jax.ShapeDtypeStruct((conts,), F32),
-        ),
+        out_shape=jax.ShapeDtypeStruct((8, HD), F32),
         in_specs=[smem_spec] * 4 + [vmem_spec] * 3 + [any_spec] * 7,
-        out_specs=(vmem_spec, smem_spec, smem_spec),
+        out_specs=vmem_spec,
         scratch_shapes=[
             pltpu.VMEM((heads, 2, prompts, positions, HD), BF16),
             pltpu.VMEM((2, prompts, n * positions, HD), BF16),
@@ -808,6 +810,7 @@
             pltpu.VMEM((CHUNKS, n * own, per_head * HD), BF16),
             pltpu.VMEM((CHUNKS, n * feats, chunk_rows), BF16),
             pltpu.VMEM((feats, features), BF16),
+            pltpu.VMEM((1, n * feats), F32),
             pltpu.VMEM((vmem_rows, n * feats), BF16),
             pltpu.VMEM((2, HD), F32),
             pltpu.VMEM((n, 2, HD), F32),
@@ -859,7 +862,7 @@
     group_of,
     rewards,
 ):
-    return scores_of(
+    found = scores_of(
         n,
         group_of,
         prompt_len,
@@ -867,7 +870,7 @@
         cont_len,
         group_of.reshape(1, -1),
         target_ids,
-        norm_gain.reshape(1, -1),
+        norm_gain.reshape(-1, HD),
         cont_query,
         cont_key,
         cont_value,
@@ -876,6 +879,8 @@
         out_weight.T,
         lm_head.T,
     )
+    conts, span, _ = cont_query.shape
+    return (found[:conts, :span], found[conts, :conts], found[conts + 1, :conts])
 
 
 def solution(mesh):

time: 240 us -> 238 us (level)
    unnamed x3 -> x0, local copies, waits for them, and re-layouts: 3.54 us -> none
where the time goes in v5:
time: 238 us; the launch traced here: 237 us
  Pallas kernels  234 us (98%)
  local copies, waits for them, and re-layouts  2.5 us (1%)
    pallas_call x1, Pallas kernels, scores_of(): pl.pallas_call(functools.partial(kernel, dims), out_shape=jax.ShapeDtypeS...  234 us

profile of v5, /device:TPU:69, one launch (start us, length us, event | category | flops | bytes accessed | tf_op | source)
XLA Modules:
  0.0 237.4 jit_solution(10738423453442210936)
XLA Ops:
  0.6 234.3 %scores.1 = f32[8,128]{1,0:T(8,128)} custom-call(s32[64]{0:T(128)} %group_of.1, s32[4]{0:T(128)} %prompt_len.1, f32[2]{0:T(128)} %rewards.1, s32[2]{0:T(128)} %cont_len.1, s32[1,64]{1,0:T(1,128)} %bitcast.11, s32[2,32]{1,0:T(2,128)} %ids.1, f32[20,128]{1,0:T(8,128)} %bitcast.10, bf16[2,32,2560]{2,1,0:T(8,128)(2,1)} %q.1, bf16[2,32,512]{2,1,0:T(8,128)(2,1)} %ck.1, ...), custom_call_target="tpu_custom_call" | custom-call | tf_op jit(solution)/shard_map/scores/pallas_call | solution.py:800
  234.9 1.3 slice_bitcast_fusion
  236.2 1.2 slice.9

commit v6 on v5

--- a/solution.py
+++ b/solution.py
@@ -17,9 +17,9 @@
 CORES = 2
 CHUNKS = 4
 STARTS = (0, 0, 5, 7)
-PER_SLOT = 2
-TILE = 480
-PIECES = 3
+PER_SLOT = 1
+TILE = 800
+PIECES = 5
 WEIGH = 160
 HALF = 8
 

time: 238 us -> 239 us (level)
  no operation moved by 1% of the time
where the time goes in v6:
time: 239 us; the launch traced here: 238 us
  Pallas kernels  235 us (98%)
  local copies, waits for them, and re-layouts  2.5 us (1%)
    pallas_call x1, Pallas kernels, scores_of(): pl.pallas_call(functools.partial(kernel, dims), out_shape=jax.ShapeDtypeS...  235 us

profile of v6, /device:TPU:69, one launch (start us, length us, event | category | flops | bytes accessed | tf_op | source)
XLA Modules:
  0.0 238.4 jit_solution(5534956214176533916)
XLA Ops:
  0.6 235.2 %scores.1 = f32[8,128]{1,0:T(8,128)} custom-call(s32[64]{0:T(128)} %group_of.1, s32[4]{0:T(128)} %prompt_len.1, f32[2]{0:T(128)} %rewards.1, s32[2]{0:T(128)} %cont_len.1, s32[1,64]{1,0:T(1,128)} %bitcast.11, s32[2,32]{1,0:T(2,128)} %ids.1, f32[20,128]{1,0:T(8,128)} %bitcast.10, bf16[2,32,2560]{2,1,0:T(8,128)(2,1)} %q.1, bf16[2,32,512]{2,1,0:T(8,128)(2,1)} %ck.1, ...), custom_call_target="tpu_custom_call" | custom-call | tf_op jit(solution)/shard_map/scores/pallas_call | solution.py:800
  235.9 1.3 slice_bitcast_fusion
  237.2 1.2 slice.9
